TPU v7x, 32 devices: a whole 2x2x4 slice. The times are simulated.
32 devices in a mesh: shard: 32 (over z, y, x, core).
Axes of the slice: x: 2, y: 2, z: 4, core: 2. Of those that a mesh axis runs over, the one named last changes fastest.
Arguments:
- data_t: bfloat16 [8192, 8192], P('shard'), may hold values from -0.125 to 0.125
- labels: int32 [8192], replicated, may hold values from -1 to 1, as said below
- sample_weight: float32 [8192], replicated, may hold values from 0.1 to 4
- w_start: float32 [8192], P('shard'), may hold values from -10 to 10
- alpha_start: float32 [8192], P('shard'), may hold values from 0 to 1
- visit_order: int32 [64, 128], P('shard'), may hold values from 0 to 127, each once within a row
Outputs:
- weights_out: float32 [8192], P('shard')
- alpha_final: float32 [8192], P('shard')
- objective: float32 [], replicated
Inputs may be any that keep to these rules, and one draw needn't show every extreme that they name: `labels`: each label is -1 or +1. `visit_order`: each row is a permutation of 0 to 127.
All inputs are finite; a program needn't handle non-finite values.
Results may differ from a plain program's by a relative error of at most 0.0047.
Values may be sent and summed in bfloat16 or wider, within the bound.
A program may use at most 64 MiB of HBM per device.

v0:
```python
import jax
import jax.numpy as jnp
from jax import lax
from jax.sharding import PartitionSpec as P

GROUP = 16


def sweep_rows(gram_block, label_rows, bound_rows, alpha_rows, margin_rows, visit_rows):
    gram_perm = gram_block[visit_rows][:, visit_rows]
    label_perm = label_rows[visit_rows]
    bound_perm = bound_rows[visit_rows]
    alpha_perm = alpha_rows[visit_rows]
    margin_perm = margin_rows[visit_rows]
    diag_perm = jnp.diagonal(gram_perm) + 1e-06

    def update_group(group_index, state_pair):
        alpha_now, margin_now = state_pair
        first_row = jnp.asarray(group_index * GROUP).astype(jnp.int32)
        group_alpha = lax.dynamic_slice_in_dim(alpha_now, first_row, GROUP)
        group_label = lax.dynamic_slice_in_dim(label_perm, first_row, GROUP)
        group_margin = lax.dynamic_slice_in_dim(margin_now, first_row, GROUP)
        group_diag = lax.dynamic_slice_in_dim(diag_perm, first_row, GROUP)
        group_bound = lax.dynamic_slice_in_dim(bound_perm, first_row, GROUP)
        fresh_alpha = jnp.clip(
            group_alpha + (1.0 - group_label * group_margin) / (2.0 * group_diag), 0.0, group_bound
        )
        change = fresh_alpha - group_alpha
        columns = lax.dynamic_slice_in_dim(gram_perm, first_row, GROUP, 1)
        margin_now = margin_now + 2.0 * jnp.dot(
            columns, group_label * change, precision=lax.Precision.HIGHEST
        )
        alpha_now = lax.dynamic_update_slice_in_dim(alpha_now, fresh_alpha, first_row, 0)
        return (alpha_now, margin_now)

    alpha_perm, margin_perm = lax.fori_loop(
        0, alpha_rows.shape[0] // GROUP, update_group, (alpha_perm, margin_perm)
    )
    return jnp.zeros_like(alpha_rows).at[visit_rows].set(alpha_perm)


def body(data_t, labels, sample_weight, w_start, alpha_start, visit_order):
    device_index = lax.axis_index("shard")
    devices = lax.axis_size("shard")
    local_feat = data_t.shape[0]
    samples = labels.shape[0]
    row_count = alpha_start.shape[0]
    features = local_feat * devices
    label_sign = labels.astype(jnp.float32)
    row_first = device_index * row_count
    own_signs = lax.dynamic_slice_in_dim(label_sign, row_first, row_count)
    own_bound = lax.dynamic_slice_in_dim(sample_weight, row_first, row_count)
    relaid = lax.all_to_all(data_t, "shard", split_axis=1, concat_axis=0, tiled=True)
    start_part = jnp.dot(w_start.astype(jnp.bfloat16), data_t, preferred_element_type=jnp.float32)
    start_margin = lax.psum(start_part, "shard")
    weighted = (
        sample_weight * label_sign * jnp.maximum(0.0, 1.0 - label_sign * start_margin)
    ).astype(jnp.bfloat16)
    ascent = jnp.dot(data_t, weighted, preferred_element_type=jnp.float32)
    column_sq = jnp.einsum("fs,fs->f", data_t, data_t, preferred_element_type=jnp.float32)
    scale_col = column_sq / samples + 1e-06
    stepped = w_start + ascent / (samples * scale_col)
    thresh = 1.0 / (4.0 * features * scale_col)
    primal = stepped - jnp.clip(stepped, -thresh, thresh)
    model_part = jnp.dot(primal.astype(jnp.bfloat16), data_t, preferred_element_type=jnp.float32)
    penalty_part = jnp.sum(jnp.abs(primal)) / (4.0 * features)
    own_margin = lax.psum_scatter(model_part, "shard", scatter_dimension=0, tiled=True)
    loss_part = jnp.sum(own_bound * jnp.square(jnp.maximum(0.0, 1.0 - own_signs * own_margin))) / (
        2.0 * samples
    )
    loss_total, penalty = lax.psum((loss_part, penalty_part), "shard")
    objective = loss_total + penalty
    gram_block = lax.dot_general(
        relaid, relaid, (((0,), (0,)), ((), ())), preferred_element_type=jnp.float32
    )
    block_count = visit_order.shape[0]
    visit_rows = (
        visit_order + (jnp.arange(block_count, dtype=jnp.int32) * visit_order.shape[1])[:, None]
    ).reshape(row_count)
    alpha_zero = own_bound * alpha_start
    alpha_one = sweep_rows(gram_block, own_signs, own_bound, alpha_zero, own_margin, visit_rows)
    change_one = (own_signs * (alpha_one - alpha_zero)).astype(jnp.bfloat16)
    update_part = jnp.dot(relaid, change_one, preferred_element_type=jnp.float32) * (2.0 / devices)
    update_one = lax.psum(update_part, "shard")
    second_margin = own_margin + jnp.dot(
        update_one.astype(jnp.bfloat16), relaid, preferred_element_type=jnp.float32
    )
    alpha_two = sweep_rows(gram_block, own_signs, own_bound, alpha_one, second_margin, visit_rows)
    change_two = (own_signs * (alpha_two - alpha_one)).astype(jnp.bfloat16)
    second_part = jnp.dot(relaid, change_two, preferred_element_type=jnp.float32) * (2.0 / devices)
    feat_first = device_index * local_feat
    update_two = lax.psum(second_part, "shard")
    own_two = lax.dynamic_slice_in_dim(update_two, feat_first, local_feat)
    own_one = lax.dynamic_slice_in_dim(update_one, feat_first, local_feat)
    return (primal + own_one + own_two, alpha_two, objective)


def solution(mesh):
    placed = (P("shard", None), P(), P(), P("shard"), P("shard"), P("shard", None))
    return jax.shard_map(
        body, mesh=mesh, in_specs=placed, out_specs=(P("shard"), P("shard"), P()), check_vma=False
    )
```

profile of v0, /device:TPU:14, one launch (start us, length us, event | category | flops | bytes accessed | tf_op | source)
XLA Modules:
  0.0 315.5 jit_solution(12440864550533348112)
XLA Ops:
  0.6 6.4 %copy.19 = bf16[256,8192]{0,1:T(8,128)(2,1)} copy(bf16[256,8192]{1,0:T(8,128)(2,1)} %param.10) | data formatting | bytes 8388608 | tf_op args[0]
  7.0 6.4 %copy.20 = bf16[256,32,256]{2,0,1:T(8,128)(2,1)} copy(bf16[256,32,256]{0,2,1:T(8,128)(2,1)} %bitcast.48) | data formatting | bytes 8388608 | tf_op jit(solution)/shard_map/all_to_all | solution.py:53
  13.4 6.0 %all-to-all-start = ((bf16[256,32,256]{2,0,1:T(8,128)(2,1)}), bf16[256,32,256]{2,0,1:T(8,128)(2,1)}, u32[]{:S(2)}, u32[]{:S(2)}) async-start(bf16[256,32,256]{2,0,1:T(8,128)(2,1)} %copy.20), calls=%async_computation | async-start | bytes 8388608 | tf_op jit(solution)/shard_map/all_to_all | solution.py:53
  19.5 2.8 fusion.28
  22.4 109.1 %psum.35 = f32[8192]{0:T(1024)S(1)} all-reduce(f32[8192]{0:T(1024)S(1)} %bitcast.53), channel_id=1, replica_groups=mesh['shard'=32] {'shard'}, use_global_device_ids=true, to_apply=%region_0.0 | all-reduce | flops 8192 | bytes 65536 | tf_op jit(solution)/shard_map/psum | solution.py:55
  131.5 3.5 %fusion.29 = f32[1,256]{1,0:T(1,128)S(1)} fusion(bf16[8192,1]{0,1:T(2,128)(2,1)S(1)} %reshape.137, bf16[256,8192]{1,0:T(8,128)(2,1)} %param.10), kind=kOutput, calls=%fused_computation.58 | convolution fusion | flops 4194304 | bytes 4211712 | tf_op jit(solution)/shard_map/dot_general | solution.py:59
  136.6 2.8 fusion.30
  139.5 42.1 %all-reduce = f32[8192]{0:T(1024)S(1)} all-reduce(f32[8192]{0:T(1024)S(1)} %bitcast.54), channel_id=2, replica_groups=mesh['shard'=32] {'shard'}, use_global_device_ids=true, to_apply=%region_1.2.clone | all-reduce | flops 8192 | bytes 65536
  182.3 1.9 gather_fusion.3
  184.3 1.9 gather_fusion.2
  186.3 1.9 gather_fusion
  188.2 1.9 gather_fusion.1
  191.5 4.7 %fusion.19 = f32[256,256]{1,0:T(8,128)S(1)} fusion(bf16[256,32,256]{2,0,1:T(8,128)(2,1)} %all-to-all-done), kind=kOutput, calls=%fused_computation.35 | convolution fusion | flops 1073741824 | bytes 4456448 | tf_op jit(solution)/shard_map/dot_general | solution.py:73
  198.5 2.4 gather_fusion.6
  200.8 8.5 %while.30 = (s32[]{:T(128)}, f32[256]{0:T(256)S(1)}, f32[256]{0:T(256)S(1)}, f32[256]{0:T(256)S(1)}, f32[256]{0:T(256)S(1)}, /*index=5*/f32[256]{0:T(256)S(1)}, ...) while((s32[]{:T(128)}, f32[256]{0:T(256)S(1)}, f32[256]{0:T(256)S(1)}, ...), condition=%wide.region_3.4_spmd, body=%wide.region_2.3_spmd.sunk | while | flops 49814 | bytes 145567 | solution.py:36
  210.7 1.9 gather_fusion.7
  212.7 3.4 %fusion.31 = f32[1,8192]{1,0:T(1,128)S(1)} fusion(bf16[256,1]{0,1:T(2,128)(2,1)S(1)} %reshape.144, bf16[8192,256]{1,0:T(8,128)(2,1)} %bitcast.14), kind=kOutput, calls=%fused_computation.60 | convolution fusion | flops 4194304 | bytes 4227584 | tf_op jit(solution)/shard_map/dot_general | solution.py:83
  216.1 38.4 %psum.36 = f32[8192]{0:T(1024)S(1)} all-reduce(f32[8192]{0:T(1024)S(1)} %broadcast_multiply_fusion.1), channel_id=1, replica_groups=mesh['shard'=32] {'shard'}, use_global_device_ids=true, to_apply=%region_5.6 | all-reduce | flops 8192 | bytes 65536 | tf_op jit(solution)/shard_map/psum | solution.py:84
  254.5 2.8 fusion.32
  257.4 2.0 gather_fusion.8
  259.3 8.5 %while.31 = (s32[]{:T(128)}, f32[256]{0:T(256)S(1)}, f32[256]{0:T(256)S(1)}, f32[256]{0:T(256)S(1)}, f32[256]{0:T(256)S(1)}, /*index=5*/f32[256]{0:T(256)S(1)}, ...) while((s32[]{:T(128)}, f32[256]{0:T(256)S(1)}, f32[256]{0:T(256)S(1)}, ...), condition=%wide.region_7.8_spmd, body=%wide.region_6.7_spmd.sunk | while | flops 49814 | bytes 145567 | solution.py:36
  267.8 1.4 scatter_custom_fusion.1
  269.2 3.4 %fusion.33 = f32[1,8192]{1,0:T(1,128)S(1)} fusion(bf16[256,1]{0,1:T(2,128)(2,1)S(1)} %reshape.148, bf16[8192,256]{1,0:T(8,128)(2,1)} %bitcast.14), kind=kOutput, calls=%fused_computation.62 | convolution fusion | flops 4194304 | bytes 4227584 | tf_op jit(solution)/shard_map/dot_general | solution.py:90
  272.6 42.2 %all-reduce.1 = (f32[8192]{0:T(1024)S(1)}, f32[]{:T(128)}) all-reduce(f32[8192]{0:T(1024)S(1)} %broadcast_multiply_fusion, f32[]{:T(128)S(6)} %add.173), channel_id=1, replica_groups=mesh['shard'=32] {'shard'}, use_global_device_ids=true, to_apply=%region_9.10 | all-reduce | flops 8193 | bytes 65544 | tf_op jit(solution)/shard_map/psum | solution.py:92
  (207 shorter events, 22.2 us)
Async XLA Ops:
  13.4 6.1 %copy-start.6 = (f32[256]{0:T(256)S(1)}, f32[256]{0:T(256)}, u32[]{:S(2)}) copy-start(f32[256]{0:T(256)} %param.13) | copy-start | bytes 3076
  13.4 6.1 %copy-start.1 = (s32[8192]{0:T(1024)S(1)}, s32[8192]{0:T(1024)}, u32[]{:S(2)}) copy-start(s32[8192]{0:T(1024)} %param.11) | copy-start | bytes 98308
  13.4 178.0 %all-to-all-start = ((bf16[256,32,256]{2,0,1:T(8,128)(2,1)}), bf16[256,32,256]{2,0,1:T(8,128)(2,1)}, u32[]{:S(2)}, u32[]{:S(2)}) async-start(bf16[256,32,256]{2,0,1:T(8,128)(2,1)} %copy.20), calls=%async_computation | async-start | bytes 8388608 | tf_op jit(solution)/shard_map/all_to_all | solution.py:53
  19.5 112.0 %copy-start.2 = (f32[8192]{0:T(1024)S(1)}, f32[8192]{0:T(1024)}, u32[]{:S(2)}) copy-start(f32[8192]{0:T(1024)} %param.12) | copy-start | bytes 98308
  131.5 3.6 %copy-start = (bf16[256,8192]{1,0:T(8,128)(2,1)S(1)}, bf16[256,8192]{1,0:T(8,128)(2,1)}, u32[]{:S(2)}) copy-start(bf16[256,8192]{1,0:T(8,128)(2,1)} %param.10) | copy-start | bytes 12582916
  135.1 47.2 %copy-start.5 = (s32[2,128]{1,0:T(2,128)S(1)}, s32[2,128]{1,0:T(2,128)}, u32[]{:S(2)}) copy-start(s32[2,128]{1,0:T(2,128)} %param.15) | copy-start | bytes 3076
  136.0 50.2 %copy-start.3 = (f32[256]{0:T(256)S(1)}, f32[256]{0:T(256)}, u32[]{:S(2)}) copy-start(f32[256]{0:T(256)} %param.14) | copy-start | bytes 3076
  269.2 46.3 %copy-start.4 = (f32[256]{0:T(256)}, f32[256]{0:T(256)S(1)}, u32[]{:S(2)}) copy-start(f32[256]{0:T(256)S(1)} %scatter_custom_fusion.1) | copy-start | bytes 3076
where the time goes:
time: 316 us; the launch traced here: 315 us
  blocking collectives  232 us (73%)
  local copies, waits for them, and re-layouts  32.1 us (10%)
  matrix products  31.5 us (10%)
  other arithmetic  10.4 us (3%)
  starting transfers between devices  6.02 us (2%)
    psum x1, blocking collectives, body(): start_margin = lax.psum(start_part, 'shard')  109 us
    psum x1, blocking collectives, body(): update_two = lax.psum(second_part, 'shard')  42.2 us
    unnamed x1, blocking collectives  42.1 us
    psum x1, blocking collectives, body(): update_one = lax.psum(update_part, 'shard')  38.4 us
    dot_general x32, matrix products, update_group(): jnp.dot(columns, group_label * change, precision=lax.Precision.HIGHEST)  7.97 us
    unnamed x15, local copies, waits for them, and re-layouts  6.44 us
    all_to_all x1, local copies, waits for them, and re-layouts, body(): lax.all_to_all(data_t, 'shard', split_axis=1, concat_axis=0, tiled=True)  6.41 us
  transfers between devices with their start and end apart: 1, of which 0 were waited for; matrix products, arithmetic and copies ran while one was open for 6% of the time, Pallas kernels for 0%

commit v1 on v0

--- a/solution.py
+++ b/solution.py
@@ -52,7 +52,7 @@
     own_bound = lax.dynamic_slice_in_dim(sample_weight, row_first, row_count)
     relaid = lax.all_to_all(data_t, "shard", split_axis=1, concat_axis=0, tiled=True)
     start_part = jnp.dot(w_start.astype(jnp.bfloat16), data_t, preferred_element_type=jnp.float32)
-    start_margin = lax.psum(start_part, "shard")
+    start_margin = jnp.sum(lax.all_gather(start_part, axis_name="shard"), axis=0)
     weighted = (
         sample_weight * label_sign * jnp.maximum(0.0, 1.0 - label_sign * start_margin)
     ).astype(jnp.bfloat16)

time: 316 us -> 300 us (0.949)
  blocking collectives: 232 us -> 124 us
  waiting for transfers between devices: 0.01 us -> 74.6 us
  between operations: 2.28 us -> 15.7 us
    psum x1 -> x0, blocking collectives: 109 us -> none  [body(): start_margin = lax.psum(start_part, 'shard')]
    all_gather x0 -> x1, waiting for transfers between devices: none -> 74.6 us  [body(): lax.all_gather(start_part, axis_name='shard')]
  transfers between devices with their start and end apart: 1 -> 2, of which waited for: 0 -> 1; matrix products, arithmetic and copies ran while one was open for 6% -> 7% of each run, Pallas kernels for 0% -> 0%
where the time goes in v1:
time: 300 us; the launch traced here: 298 us
  blocking collectives  124 us (41%)
  waiting for transfers between devices  74.6 us (25%)
  local copies, waits for them, and re-layouts  33.5 us (11%)
  matrix products  29.9 us (10%)
  between operations  15.7 us (5%)
  other arithmetic  12.7 us (4%)
  starting transfers between devices  6.06 us (2%)
    all_gather x1, waiting for transfers between devices, body(): lax.all_gather(start_part, axis_name='shard')  74.6 us
    unnamed x1, blocking collectives  43.1 us
    psum x1, blocking collectives, body(): update_two = lax.psum(second_part, 'shard')  40.7 us
    psum x1, blocking collectives, body(): update_one = lax.psum(update_part, 'shard')  39.9 us
    dot_general x32, matrix products, update_group(): jnp.dot(columns, group_label * change, precision=lax.Precision.HIGHEST)  7.97 us
    unnamed x15, local copies, waits for them, and re-layouts  6.44 us
    all_to_all x1, local copies, waits for them, and re-layouts, body(): lax.all_to_all(data_t, 'shard', split_axis=1, concat_axis=0, tiled=True)  6.41 us
    all_to_all x1, starting transfers between devices, body(): lax.all_to_all(data_t, 'shard', split_axis=1, concat_axis=0, tiled=True)  6.02 us
  transfers between devices with their start and end apart: 2, of which 1 were waited for; matrix products, arithmetic and copies ran while one was open for 7% of the time, Pallas kernels for 0%

profile of v1, /device:TPU:14, one launch (start us, length us, event | category | flops | bytes accessed | tf_op | source)
XLA Modules:
  0.0 297.6 jit_solution(16320952864683909127)
XLA Ops:
  7.2 6.4 %copy.25 = bf16[256,8192]{0,1:T(8,128)(2,1)} copy(bf16[256,8192]{1,0:T(8,128)(2,1)} %param.10) | data formatting | bytes 8388608 | tf_op args[0]
  13.6 6.4 %copy.26 = bf16[256,32,256]{2,0,1:T(8,128)(2,1)} copy(bf16[256,32,256]{0,2,1:T(8,128)(2,1)} %bitcast.48) | data formatting | bytes 8388608 | tf_op jit(solution)/shard_map/all_to_all | solution.py:53
  20.0 6.0 %all-to-all-start = ((bf16[256,32,256]{2,0,1:T(8,128)(2,1)}), bf16[256,32,256]{2,0,1:T(8,128)(2,1)}, u32[]{:S(2)}, u32[]{:S(2)}) async-start(bf16[256,32,256]{2,0,1:T(8,128)(2,1)} %copy.26), calls=%async_computation | async-start | bytes 8388608 | tf_op jit(solution)/shard_map/all_to_all | solution.py:53
  26.1 3.4 %fusion.28 = f32[1,8192]{1,0:T(1,128)} fusion(bf16[256,1]{0,1:T(2,128)(2,1)S(1)} %reshape.136, bf16[256,8192]{1,0:T(8,128)(2,1)} %param.10), kind=kOutput, calls=%fused_computation.57 | convolution fusion | flops 4194304 | bytes 4227584 | tf_op jit(solution)/shard_map/dot_general | solution.py:54
  29.7 3.1 %fusion.16 = f32[256]{0:T(256)S(1)} fusion(bf16[256,8192]{1,0:T(8,128)(2,1)} %param.10), kind=kLoop, calls=%fused_computation.32 | loop fusion | flops 6291200 | bytes 4195328 | tf_op jit(solution)/shard_map/fs,fs->f/dot_general | solution.py:60
  32.8 74.6 %all-gather.3.cloned.1.call-done = f32[262144]{0:T(1024)} async-done(((f32[8192]{0:T(1024)}), f32[262144]{0:T(1024)}) %all-gather.3.cloned.1.call-update) | async-done | bytes 1048592 | tf_op jit(solution)/shard_map/all_gather | solution.py:55
  107.4 1.4 reshape.131
  109.0 3.5 %fusion.29 = f32[1,256]{1,0:T(1,128)S(1)} fusion(bf16[8192,1]{0,1:T(2,128)(2,1)S(1)} %reshape.138, bf16[256,8192]{1,0:T(8,128)(2,1)} %param.10), kind=kOutput, calls=%fused_computation.58 | convolution fusion | flops 4194304 | bytes 4211712 | tf_op jit(solution)/shard_map/dot_general | solution.py:59
  113.9 43.1 %all-reduce = f32[8192]{0:T(1024)S(1)} all-reduce(f32[8192]{0:T(1024)S(1)} %bitcast.54), channel_id=3, replica_groups=mesh['shard'=32] {'shard'}, use_global_device_ids=true, to_apply=%region_1.2.clone | all-reduce | flops 8192 | bytes 65536
  157.6 1.9 gather_fusion.3
  159.6 1.9 gather_fusion.2
  161.5 1.9 gather_fusion
  163.5 1.9 gather_fusion.1
  166.8 4.7 %fusion.19 = f32[256,256]{1,0:T(8,128)S(1)} fusion(bf16[256,32,256]{2,0,1:T(8,128)(2,1)} %all-to-all-done), kind=kOutput, calls=%fused_computation.35 | convolution fusion | flops 1073741824 | bytes 4456448 | tf_op jit(solution)/shard_map/dot_general | solution.py:73
  173.7 2.4 gather_fusion.6
  176.1 8.5 %while.30 = (s32[]{:T(128)}, f32[256]{0:T(256)S(1)}, f32[256]{0:T(256)S(1)}, f32[256]{0:T(256)S(1)}, f32[256]{0:T(256)S(1)}, /*index=5*/f32[256]{0:T(256)S(1)}, ...) while((s32[]{:T(128)}, f32[256]{0:T(256)S(1)}, f32[256]{0:T(256)S(1)}, ...), condition=%wide.region_3.4_spmd, body=%wide.region_2.3_spmd.sunk | while | flops 49814 | bytes 145567 | solution.py:36
  186.0 1.9 gather_fusion.7
  188.0 3.4 %fusion.31 = f32[1,8192]{1,0:T(1,128)S(1)} fusion(bf16[256,1]{0,1:T(2,128)(2,1)S(1)} %reshape.145, bf16[8192,256]{1,0:T(8,128)(2,1)} %bitcast.14), kind=kOutput, calls=%fused_computation.60 | convolution fusion | flops 4194304 | bytes 4227584 | tf_op jit(solution)/shard_map/dot_general | solution.py:83
  191.3 39.9 %psum.28 = f32[8192]{0:T(1024)S(1)} all-reduce(f32[8192]{0:T(1024)S(1)} %broadcast_multiply_fusion.1), channel_id=1, replica_groups=mesh['shard'=32] {'shard'}, use_global_device_ids=true, to_apply=%region_5.6 | all-reduce | flops 8192 | bytes 65536 | tf_op jit(solution)/shard_map/psum | solution.py:84
  231.3 2.8 fusion.32
  234.2 2.0 gather_fusion.8
  236.1 8.5 %while.31 = (s32[]{:T(128)}, f32[256]{0:T(256)S(1)}, f32[256]{0:T(256)S(1)}, f32[256]{0:T(256)S(1)}, f32[256]{0:T(256)S(1)}, /*index=5*/f32[256]{0:T(256)S(1)}, ...) while((s32[]{:T(128)}, f32[256]{0:T(256)S(1)}, f32[256]{0:T(256)S(1)}, ...), condition=%wide.region_7.8_spmd, body=%wide.region_6.7_spmd.sunk | while | flops 49814 | bytes 145567 | solution.py:36
  246.1 3.4 %fusion.33 = f32[1,8192]{1,0:T(1,128)S(1)} fusion(bf16[256,1]{0,1:T(2,128)(2,1)S(1)} %reshape.149, bf16[8192,256]{1,0:T(8,128)(2,1)} %bitcast.14), kind=kOutput, calls=%fused_computation.62 | convolution fusion | flops 4194304 | bytes 4227584 | tf_op jit(solution)/shard_map/dot_general | solution.py:90
  249.4 40.7 %all-reduce.1 = (f32[8192]{0:T(1024)S(1)}, f32[]{:T(128)}) all-reduce(f32[8192]{0:T(1024)S(1)} %broadcast_multiply_fusion, f32[]{:T(128)S(6)} %add.171), channel_id=1, replica_groups=mesh['shard'=32] {'shard'}, use_global_device_ids=true, to_apply=%region_9.10 | all-reduce | flops 8193 | bytes 65544 | tf_op jit(solution)/shard_map/psum | solution.py:92
  (211 shorter events, 23.5 us)
Async XLA Ops:
  20.0 6.1 %copy-start.6 = (f32[256]{0:T(256)S(1)}, f32[256]{0:T(256)}, u32[]{:S(2)}) copy-start(f32[256]{0:T(256)} %param.13) | copy-start | bytes 3076
  20.0 146.8 %all-to-all-start = ((bf16[256,32,256]{2,0,1:T(8,128)(2,1)}), bf16[256,32,256]{2,0,1:T(8,128)(2,1)}, u32[]{:S(2)}, u32[]{:S(2)}) async-start(bf16[256,32,256]{2,0,1:T(8,128)(2,1)} %copy.26), calls=%async_computation | async-start | bytes 8388608 | tf_op jit(solution)/shard_map/all_to_all | solution.py:53
  26.0 3.6 %copy-start.1 = (s32[8192]{0:T(1024)S(1)}, s32[8192]{0:T(1024)}, u32[]{:S(2)}) copy-start(s32[8192]{0:T(1024)} %param.11) | copy-start | bytes 98308
  26.0 3.6 %copy-start.5 = (s32[2,128]{1,0:T(2,128)S(1)}, s32[2,128]{1,0:T(2,128)}, u32[]{:S(2)}) copy-start(s32[2,128]{1,0:T(2,128)} %param.15) | copy-start | bytes 3076
  26.0 81.4 %all-gather.3.cloned.1.call-start = ((), (), s32[]{:S(2)}) async-start(), calls=%async_computation.1 | async-start | bytes 1081344 | tf_op jit(solution)/shard_map/all_gather | solution.py:55
  29.6 79.4 %copy-start.2 = (f32[8192]{0:T(1024)S(1)}, f32[8192]{0:T(1024)}, u32[]{:S(2)}) copy-start(f32[8192]{0:T(1024)} %param.12) | copy-start | bytes 98308
  109.0 4.2 %copy-start = (bf16[256,8192]{1,0:T(8,128)(2,1)S(1)}, bf16[256,8192]{1,0:T(8,128)(2,1)}, u32[]{:S(2)}) copy-start(bf16[256,8192]{1,0:T(8,128)(2,1)} %param.10) | copy-start | bytes 12582916
  112.6 49.0 %copy-start.3 = (f32[256]{0:T(256)S(1)}, f32[256]{0:T(256)}, u32[]{:S(2)}) copy-start(f32[256]{0:T(256)} %param.14) | copy-start | bytes 3076
  246.0 44.7 %copy-start.4 = (f32[256]{0:T(256)}, f32[256]{0:T(256)S(1)}, u32[]{:S(2)}) copy-start(f32[256]{0:T(256)S(1)} %scatter_custom_fusion.1) | copy-start | bytes 3076
Sparse Core Ops, SparseCore 0:
  29.7 77.6 all-gather.2
